TPU v7x, 32 devices: a whole 2x2x4 slice. The times are simulated.
32 devices in a mesh: row: 8 (over z, core), col: 4 (over y, x).
Axes of the slice: x: 2, y: 2, z: 4, core: 2. Of those that a mesh axis runs over, the one named last changes fastest.
Arguments:
- factor: bfloat16 [8192, 8192], P('row', 'col'), as said below
- sel_tiles: int32 [32], replicated, may hold values from 0 to 63, as said below
- coupling: bfloat16 [8192, 2048], P('col', 'row')
Outputs:
- root_inverse: float32 [8192, 8192], P('row', 'col')
- child_inverse: float32 [2048, 8192], P('col', 'row')
Inputs may be any that keep to these rules, and one draw needn't show every extreme that they name: sel_tiles holds 32 distinct tile indices in increasing order; rows of coupling outside the listed tiles are zero. factor is lower triangular with a diagonal between 1 and 1.5.
All inputs are finite; a program needn't handle non-finite values.
Results may differ from a plain program's by a relative error of at most 0.003.
Values may be sent and summed in bfloat16 or wider, within the bound.
A program may use at most 128 MiB of HBM per device.

v0:
```python
import jax
import jax.numpy as jnp
from jax import lax
from jax.sharding import PartitionSpec as P

TILE = 128


def from_root(value, axis, source):
    kept = jnp.where(lax.axis_index(axis) == source, value, 0).astype(value.dtype)
    return lax.psum(kept, axis)


def body(factor, sel_tiles, coupling):
    rows_here = factor.shape[0]
    row_index = lax.axis_index("row")
    whole = lax.all_gather(factor, "row", axis=0, tiled=True)
    ratio = lax.axis_size("row") // lax.axis_size("col")
    offset = row_index % ratio * rows_here
    piece = lax.dynamic_slice_in_dim(whole, offset, rows_here, 1)
    partner = from_root(piece, "col", row_index // ratio)
    gram = lax.dot_general(
        partner, whole, (((0,), (0,)), ((), ())), preferred_element_type=jnp.float32
    )
    coupling_full = lax.all_gather(coupling, "row", axis=1, tiled=True)
    rounded = gram.astype(jnp.bfloat16)
    global_rows = row_index * rows_here + jnp.arange(rows_here, dtype=jnp.int32)
    member = jnp.any((global_rows // TILE)[:, None] == sel_tiles[None, :], axis=1)
    summed = lax.psum_scatter(
        lax.dot_general(
            coupling_full, rounded, (((0,), (1,)), ((), ())), preferred_element_type=jnp.float32
        ),
        "col",
        scatter_dimension=0,
        tiled=True,
    )
    child = jnp.where(member[None, :], -summed, jnp.float32(0.0))
    return (gram, child)


def solution(mesh):
    placed = (P("row", "col"), P(), P("col", "row"))
    return jax.shard_map(
        body,
        mesh=mesh,
        in_specs=placed,
        out_specs=(P("row", "col"), P("col", "row")),
        check_vma=False,
    )
```

profile of v0, /device:TPU:0, one launch (start us, length us, event | category | flops | bytes accessed | tf_op | source)
XLA Modules:
  0.0 817.3 jit_solution(11417977400386051904)
XLA Ops:
  7.2 0.0 all-gather.3.cloned.1.call-start
  7.2 0.7 all-gather.3.cloned.1.call-update
  7.9 0.0 all-reduce.2.cloned.1.call-start
  8.0 293.0 %all-gather.3.cloned.1.call-done = bf16[8192,2048]{1,0:T(8,128)(2,1)} async-done(((bf16[1024,2048]{1,0:T(8,128)(2,1)}), bf16[8192,2048]{1,0:T(8,128)(2,1)}) %all-gather.3.cloned.1.call-update) | async-done | bytes 33554448 | tf_op jit(solution)/shard_map/all_gather | solution.py:17
  300.9 15.0 %dynamic-slice_select_fusion = bf16[8192,1024]{1,0:T(8,128)(2,1)} fusion(bf16[8192,2048]{1,0:T(8,128)(2,1)} %all-gather.3.cloned.1.call-done, s32[]{:T(128)S(6)} %select_n.38, pred[]{:T(512)S(6)} %eq.18), kind=kLoop, calls=%fused_computation | loop fusion | flops 8388608 | bytes 33554436 | tf_op jit(solution)/shard_map/jit(_where)/select_n | solution.py:10
  316.0 0.0 all-reduce.2.cloned.1.call-update
  316.0 0.0 all-gather.5.cloned.1.call-start
  316.0 0.7 all-gather.5.cloned.1.call-update
  316.7 0.0 reduce-scatter.2.cloned.1.call-start
  316.8 304.9 %all-reduce.2.cloned.1.call-done = bf16[8192,1024]{1,0:T(8,128)(2,1)} async-done(((bf16[8192,1024]{1,0:T(8,128)(2,1)}), bf16[8192,1024]{1,0:T(8,128)(2,1)}) %all-reduce.2.cloned.1.call-update) | async-done | bytes 16777232 | tf_op jit(solution)/shard_map/psum | solution.py:11
  621.7 43.9 %fusion.4 = f32[1024,2048]{1,0:T(8,128)} fusion(bf16[8192,1024]{1,0:T(8,128)(2,1)} %all-reduce.2.cloned.1.call-done, bf16[8192,2048]{1,0:T(8,128)(2,1)} %all-gather.3.cloned.1.call-done), kind=kOutput, calls=%fused_computation.14 | convolution fusion | flops 34359738368 | bytes 58720256 | tf_op jit(solution)/shard_map/dot_general | solution.py:22
  665.6 41.2 %all-gather.5.cloned.1.call-done = bf16[2048,2048]{1,0:T(8,128)(2,1)} async-done(((bf16[2048,256]{1,0:T(8,128)(2,1)}), bf16[2048,2048]{1,0:T(8,128)(2,1)}) %all-gather.5.cloned.1.call-update) | async-done | bytes 8388624 | tf_op jit(solution)/shard_map/all_gather | solution.py:25
  706.8 15.6 %convolution_bitcast_fusion = f32[2048,1024]{0,1:T(8,128)} fusion(bf16[2048,2048]{1,0:T(8,128)(2,1)} %all-gather.5.cloned.1.call-done, f32[1024,2048]{1,0:T(8,128)} %fusion.4), kind=kOutput, calls=%fused_computation.1 | convolution fusion | flops 8592031744 | bytes 25165824 | tf_op jit(solution)/shard_map/dot_general | solution.py:30
  722.4 0.0 copy-start
  722.4 0.0 reduce-scatter.2.cloned.1.call-update
  722.5 0.6 copy-done
  723.1 0.1 compare_reduce_fusion
  723.2 83.9 %reduce-scatter.2.cloned.1.call-done = f32[512,1024]{0,1:T(8,128)} async-done(((f32[2048,1024]{0,1:T(8,128)}), f32[512,1024]{0,1:T(8,128)}) %reduce-scatter.2.cloned.1.call-update) | async-done | bytes 2097168 | tf_op jit(solution)/shard_map/reduce_scatter | solution.py:29
  807.1 1.9 negate_select_fusion
  809.0 1.8 copy.6
  (1 shorter events, 0.0 us)
Async XLA Ops:
  7.2 293.8 %all-gather.3.cloned.1.call-start = ((), (), s32[]{:S(2)}) async-start(), calls=%async_computation.1 | async-start | bytes 37748736 | tf_op jit(solution)/shard_map/all_gather | solution.py:17
  7.9 613.8 %all-reduce.2.cloned.1.call-start = ((), (), s32[]{:S(2)}) async-start(), calls=%async_computation.2 | async-start | bytes 33554432 | tf_op jit(solution)/shard_map/psum | solution.py:11
  316.0 390.8 %all-gather.5.cloned.1.call-start = ((), (), s32[]{:S(2)}) async-start(), calls=%async_computation.3 | async-start | bytes 9437184 | tf_op jit(solution)/shard_map/all_gather | solution.py:25
  316.7 490.4 %reduce-scatter.2.cloned.1.call-start = ((), (), s32[]{:S(2)}) async-start(), calls=%async_computation.4 | async-start | bytes 10485760 | tf_op jit(solution)/shard_map/reduce_scatter | solution.py:29
  722.4 0.7 copy-start
Sparse Core Ops, SparseCore 0:
  9.6 291.3 all-gather.2
  316.1 305.5 all-reduce.1
  623.3 83.5 all-gather.4
  722.6 84.4 reduce-scatter.1
where the time goes:
time: 818 us; the launch traced here: 817 us
  waiting for transfers between devices  724 us (89%)
  matrix products  59.6 us (7%)
  other arithmetic  17 us (2%)
  between operations  13.8 us (2%)
    psum x1, waiting for transfers between devices, from_root(): return lax.psum(kept, axis)  305 us
    all_gather x1, waiting for transfers between devices, body(): whole = lax.all_gather(factor, 'row', axis=0, tiled=True)  293 us
    reduce_scatter x1, waiting for transfers between devices, body(): lax.psum_scatter(lax.dot_general(coupling_full, rounded, (((0,), (1,)), (...  83.9 us
    dot_general x1, matrix products, body(): lax.dot_general(partner, whole, (((0,), (0,)), ((), ())), preferred_eleme...  43.9 us
    all_gather x1, waiting for transfers between devices, body(): coupling_full = lax.all_gather(coupling, 'row', axis=1, tiled=True)  41.2 us
  transfers between devices with their start and end apart: 4, of which 4 were waited for; matrix products, arithmetic and copies ran while one was open for 5% of the time, Pallas kernels for 0%

commit v1 on v0

--- a/solution.py
+++ b/solution.py
@@ -22,7 +22,7 @@
     gram = lax.dot_general(
         partner, whole, (((0,), (0,)), ((), ())), preferred_element_type=jnp.float32
     )
-    coupling_full = lax.all_gather(coupling, "row", axis=1, tiled=True)
+    coupling_full = jnp.concatenate(lax.all_gather(coupling, "row"), 1)
     rounded = gram.astype(jnp.bfloat16)
     global_rows = row_index * rows_here + jnp.arange(rows_here, dtype=jnp.int32)
     member = jnp.any((global_rows // TILE)[:, None] == sel_tiles[None, :], axis=1)

time: 818 us -> 848 us (1.037)
  waiting for transfers between devices: 724 us -> 745 us
  local copies, waits for them, and re-layouts: 2.42 us -> 17.6 us
    all_gather x1, waiting for transfers between devices: 41.2 us -> 66.5 us  [body(): coupling_full = jnp.concatenate(lax.all_gather(coupling, 'row'), 1)]
    reshape x0 -> x1, local copies, waits for them, and re-layouts: none -> 11.8 us  [body(): coupling_full = jnp.concatenate(lax.all_gather(coupling, 'row'), 1)]
  transfers between devices with their start and end apart: 4 -> 4, of which waited for: 4 -> 4; matrix products, arithmetic and copies ran while one was open for 5% -> 3% of each run, Pallas kernels for 0% -> 0%
where the time goes in v1:
time: 848 us
  waiting for transfers between devices  745 us (88%)
  matrix products  54.4 us (6%)
  local copies, waits for them, and re-layouts  17.6 us (2%)
  other arithmetic  17.2 us (2%)
  between operations  13.8 us (2%)
    psum x1, waiting for transfers between devices, from_root(): return lax.psum(kept, axis)  298 us
    all_gather x1, waiting for transfers between devices, body(): whole = lax.all_gather(factor, 'row', axis=0, tiled=True)  292 us
    reduce_scatter x1, waiting for transfers between devices, body(): lax.psum_scatter(lax.dot_general(coupling_full, rounded, (((0,), (1,)), (...  86.8 us
    all_gather x1, waiting for transfers between devices, body(): coupling_full = jnp.concatenate(lax.all_gather(coupling, 'row'), 1)  66.5 us
    dot_general x1, matrix products, body(): lax.dot_general(partner, whole, (((0,), (0,)), ((), ())), preferred_eleme...  43.2 us
  transfers between devices with their start and end apart: 4, of which 4 were waited for; matrix products, arithmetic and copies ran while one was open for 3% of the time, Pallas kernels for 0%

profile of v1, /device:TPU:0, one launch (start us, length us, event | category | flops | bytes accessed | tf_op | source)
XLA Modules:
  0.0 847.9 jit_solution(12625466946509591858)
XLA Ops:
  7.2 0.0 all-gather.4.cloned.1.call-start
  7.2 0.7 all-gather.4.cloned.1.call-update
  7.9 0.0 all-gather.6.cloned.1.call-start
  7.9 0.7 all-gather.6.cloned.1.call-update
  8.6 0.0 all-reduce.2.cloned.1.call-start
  8.7 292.2 %all-gather.4.cloned.1.call-done = bf16[8192,2048]{1,0:T(8,128)(2,1)} async-done(((bf16[1024,2048]{1,0:T(8,128)(2,1)}), bf16[8192,2048]{1,0:T(8,128)(2,1)}) %all-gather.4.cloned.1.call-update) | async-done | bytes 33554448 | tf_op jit(solution)/shard_map/all_gather | solution.py:17
  300.9 15.3 %dynamic-slice_select_fusion = bf16[8192,1024]{1,0:T(8,128)(2,1)} fusion(bf16[8192,2048]{1,0:T(8,128)(2,1)} %all-gather.4.cloned.1.call-done, s32[]{:T(128)S(6)} %select_n.38, pred[]{:T(512)S(6)} %eq.18), kind=kLoop, calls=%fused_computation | loop fusion | flops 8388608 | bytes 33554436 | tf_op jit(solution)/shard_map/jit(_where)/select_n | solution.py:10
  316.2 0.0 all-reduce.2.cloned.1.call-update
  316.2 0.0 reduce-scatter.2.cloned.1.call-start
  316.3 66.5 %all-gather.6.cloned.1.call-done = bf16[16384,256]{1,0:T(8,128)(2,1)} async-done(((bf16[2048,256]{1,0:T(8,128)(2,1)}), bf16[16384,256]{1,0:T(8,128)(2,1)}) %all-gather.6.cloned.1.call-update) | async-done | bytes 8388624 | tf_op jit(solution)/shard_map/all_gather | solution.py:25
  382.8 11.8 %copy.9 = bf16[2048,8,256]{0,2,1:T(8,128)(2,1)} copy(bf16[2048,8,256]{2,0,1:T(8,128)(2,1)} %bitcast.9) | data formatting | bytes 16777216 | tf_op jit(solution)/shard_map/reshape | solution.py:25
  394.6 297.7 %all-reduce.2.cloned.1.call-done = bf16[8192,1024]{1,0:T(8,128)(2,1)} async-done(((bf16[8192,1024]{1,0:T(8,128)(2,1)}), bf16[8192,1024]{1,0:T(8,128)(2,1)}) %all-reduce.2.cloned.1.call-update) | async-done | bytes 16777232 | tf_op jit(solution)/shard_map/psum | solution.py:11
  692.3 0.0 copy-start
  692.3 43.2 %fusion.4 = f32[1024,2048]{1,0:T(8,128)S(1)} fusion(bf16[8192,1024]{1,0:T(8,128)(2,1)} %all-reduce.2.cloned.1.call-done, bf16[8192,2048]{1,0:T(8,128)(2,1)} %all-gather.4.cloned.1.call-done), kind=kOutput, calls=%fused_computation.14 | convolution fusion | flops 34359738368 | bytes 58720256 | tf_op jit(solution)/shard_map/dot_general | solution.py:22
  735.5 0.0 copy-start.2
  735.5 3.4 copy-done.2
  738.9 0.0 copy-done
  738.9 11.2 %convolution_bitcast_fusion = f32[2048,1024]{0,1:T(8,128)} fusion(bf16[2048,2048]{0,1:T(8,128)(2,1)S(1)} %bitcast.10, f32[1024,2048]{1,0:T(8,128)S(1)} %fusion.4), kind=kOutput, calls=%fused_computation.1 | convolution fusion | flops 8592031744 | bytes 25165824 | tf_op jit(solution)/shard_map/dot_general | solution.py:30
  750.1 0.0 copy-start.1
  750.1 0.0 reduce-scatter.2.cloned.1.call-update
  750.1 0.6 copy-done.1
  750.7 0.1 compare_reduce_fusion
  750.8 86.8 %reduce-scatter.2.cloned.1.call-done = f32[512,1024]{0,1:T(8,128)} async-done(((f32[2048,1024]{0,1:T(8,128)}), f32[512,1024]{0,1:T(8,128)}) %reduce-scatter.2.cloned.1.call-update) | async-done | bytes 2097168 | tf_op jit(solution)/shard_map/reduce_scatter | solution.py:29
  837.6 1.9 negate_select_fusion
  839.5 1.8 copy.10
  (1 shorter events, 0.0 us)
Async XLA Ops:
  7.2 293.8 %all-gather.4.cloned.1.call-start = ((), (), s32[]{:S(2)}) async-start(), calls=%async_computation.1 | async-start | bytes 37748736 | tf_op jit(solution)/shard_map/all_gather | solution.py:17
  7.9 374.9 %all-gather.6.cloned.1.call-start = ((), (), s32[]{:S(2)}) async-start(), calls=%async_computation.4 | async-start | bytes 9437184 | tf_op jit(solution)/shard_map/all_gather | solution.py:25
  8.6 683.6 %all-reduce.2.cloned.1.call-start = ((), (), s32[]{:S(2)}) async-start(), calls=%async_computation.2 | async-start | bytes 33554432 | tf_op jit(solution)/shard_map/psum | solution.py:11
  316.2 521.4 %reduce-scatter.2.cloned.1.call-start = ((), (), s32[]{:S(2)}) async-start(), calls=%async_computation.3 | async-start | bytes 10485760 | tf_op jit(solution)/shard_map/reduce_scatter | solution.py:29
  692.3 46.7 %copy-start = (bf16[2048,8,256]{0,2,1:T(8,128)(2,1)S(1)}, bf16[2048,8,256]{0,2,1:T(8,128)(2,1)}, u32[]{:S(2)}) copy-start(bf16[2048,8,256]{0,2,1:T(8,128)(2,1)} %copy.9) | copy-start | bytes 25165828
  735.5 3.4 copy-start.2
  750.1 0.7 copy-start.1
Sparse Core Ops, SparseCore 0:
  9.6 291.3 all-gather.3
  302.5 80.2 all-gather.5
  386.4 305.8 all-reduce.1
  750.2 87.3 reduce-scatter.1
